TPU v7x, 32 devices: a whole 2x2x4 slice. The times are simulated.
32 devices in a mesh: parts: 2 (over y), group: 2 (over x), dev: 4 (over z), pair: 2 (over core).
Axes of the slice: x: 2, y: 2, z: 4, core: 2. Of those that a mesh axis runs over, the one named last changes fastest.
Arguments:
- tokens: bfloat16 [2048, 2048], P(('parts', 'group', 'dev', 'pair')), parts along dimension 0, may hold values from -6 to 6
- expert_ids: int32 [2048, 2], P(('parts', 'group', 'dev', 'pair')), parts along dimension 0, may hold values from 0 to 3, all different within a row; in each aligned block of 64 rows (0 to 63, 64 to 127, ...) at most 48 rows name the same one
- route_scores: float32 [2048, 2], P(('parts', 'group', 'dev', 'pair')), parts along dimension 0, may hold values from 0.05 to 1
- w_gate: bfloat16 [8, 2048, 384], P(('group', 'dev'), None, 'pair'), may hold values from -0.125 to 0.125
- w_up: bfloat16 [8, 2048, 384], P(('group', 'dev'), None, 'pair'), may hold values from -0.125 to 0.125
- w_down: bfloat16 [8, 2048, 384], P(('group', 'dev'), None, 'pair'), may hold values from -0.21875 to 0.21875
Outputs:
- mixed_out: bfloat16 [2048, 2048], P(('parts', 'group', 'dev', 'pair')), parts along dimension 0
There are 2 independent parts, one for each index of `parts`. A program takes and returns all parts, laid end to end along the dimension named above; an argument that names none is the same for every part. Nothing has to cross between parts.
Inputs may be any that keep to these rules, and one draw needn't show every extreme that they name: `expert_ids`: each row names 2 different experts. Within each aligned block of 64 rows (the tokens of one device) no expert is named more than 48 times, a bound that some block reaches.
All inputs are finite; a program needn't handle non-finite values.
Results may differ from a plain program's by a relative error of at most 0.0057.
Values may be sent and summed in bfloat16 or wider, within the bound.
A program may use at most 128 MiB of HBM per device.

v0:
```python
import jax
import jax.numpy as jnp
from jax import lax
from jax.sharding import PartitionSpec as P


def partner_2(x, axis, apart):
    return lax.ppermute(x, axis, [(i, i ^ 1 << apart) for i in range(lax.axis_size(axis))])


def expert_block(batch_rows, gate_piece, up_piece, down_piece):
    gate_act = jnp.dot(batch_rows, gate_piece, preferred_element_type=jnp.float32)
    up_act = jnp.dot(batch_rows, up_piece, preferred_element_type=jnp.float32)
    hidden = (jax.nn.silu(gate_act) * up_act).astype(jnp.bfloat16)
    return lax.dot_general(
        hidden, down_piece, (((1,), (1,)), ((), ())), preferred_element_type=jnp.float32
    )


def shards(tokens, expert_ids, route_scores, w_gate, w_up, w_down):
    rows_dev, features = tokens.shape
    top_count = expert_ids.shape[1]
    dest_count = lax.axis_size(("group", "dev"))
    experts = dest_count // 2
    capacity = 2 * max(1, 3 * rows_dev * top_count // (4 * experts))
    half_cap = capacity // 2
    route_weight = route_scores / jnp.sum(route_scores, axis=1, keepdims=True)
    flat_ids = expert_ids.reshape(-1)
    onehot = (flat_ids[:, None] == jnp.arange(experts, dtype=jnp.int32)[None, :]).astype(jnp.int32)
    before = jnp.cumsum(onehot, axis=0) - onehot
    rank_in = jnp.sum(before * onehot, axis=1)
    target = 2 * flat_ids + rank_in // half_cap
    position = target * half_cap + rank_in % half_cap
    owners = jnp.arange(rows_dev * top_count, dtype=jnp.int32) // top_count
    outgoing = (
        jnp.zeros((dest_count * half_cap, features), jnp.bfloat16).at[position].set(tokens[owners])
    )
    outgoing = outgoing.reshape(dest_count, half_cap, features)
    arrived = lax.all_to_all(outgoing, ("group", "dev"), split_axis=0, concat_axis=0, tiled=True)
    batch_rows = arrived.reshape(dest_count * half_cap, features)
    partner = partner_2((w_gate[0], w_up[0], w_down[0]), "dev", 0)
    gate_half = jnp.concatenate([w_gate[0], partner[0]], axis=1)
    up_half = jnp.concatenate([w_up[0], partner[1]], axis=1)
    down_half = jnp.concatenate([w_down[0], partner[2]], axis=1)
    full_gate, full_up, full_down = (
        lax.all_gather(gate_half, "pair", axis=1, tiled=True),
        lax.all_gather(up_half, "pair", axis=1, tiled=True),
        lax.all_gather(down_half, "pair", axis=1, tiled=True),
    )
    result = expert_block(batch_rows, full_gate, full_up, full_down)
    answer = result.astype(jnp.bfloat16).reshape(dest_count, half_cap, features)
    returned = lax.all_to_all(answer, ("group", "dev"), split_axis=0, concat_axis=0, tiled=True)
    picked = returned.reshape(dest_count * half_cap, features)[position].astype(jnp.float32)
    weighted = picked * route_weight.reshape(-1)[:, None]
    mixed_out = jnp.sum(weighted.reshape(rows_dev, top_count, features), axis=1)
    return mixed_out.astype(jnp.bfloat16)


def solution(mesh):
    in_specs = (
        P(("parts", "group", "dev", "pair"), None),
        P(("parts", "group", "dev", "pair"), None),
        P(("parts", "group", "dev", "pair"), None),
        P(("group", "dev"), None, "pair"),
        P(("group", "dev"), None, "pair"),
        P(("group", "dev"), None, "pair"),
    )
    out_specs = P(("parts", "group", "dev", "pair"), None)
    return jax.shard_map(shards, mesh=mesh, in_specs=in_specs, out_specs=out_specs, check_vma=False)
```

profile of v0, /device:TPU:0, one launch (start us, length us, event | category | flops | bytes accessed | tf_op | source)
XLA Modules:
  0.0 139.0 jit_solution(535136863781979926)
XLA Ops:
  6.5 3.1 %collective-permute-start = (bf16[2048,192]{0,1:T(8,128)(2,1)}, bf16[2048,192]{0,1:T(8,128)(2,1)S(1)}, u32[]{:S(2)}, u32[]{:S(2)}) collective-permute-start(bf16[2048,192]{0,1:T(8,128)(2,1)} %bitcast.41), channel_id=1, source_target_pairs={{0,2},{2,0},{4,6},{6,4},{1,3},{3,1},{5,7},{7,5},{8,10},{10,8},{12,... | collective-permute-start | bytes 2359304 | tf_op jit(solution)/shard_map/ppermute | solution.py:8
  9.6 17.7 %collective-permute-done = bf16[2048,192]{0,1:T(8,128)(2,1)S(1)} collective-permute-done((bf16[2048,192]{0,1:T(8,128)(2,1)}, bf16[2048,192]{0,1:T(8,128)(2,1)S(1)}, u32[]{:S(2)}, u32[]{:S(2)}) %collective-permute-start) | collective-permute-done | bytes 786464 | tf_op jit(solution)/shard_map/ppermute | solution.py:8
  27.3 2.4 %pad_maximum_fusion = bf16[2048,384]{0,1:T(8,128)(2,1)} fusion(bf16[2048,192]{0,1:T(8,128)(2,1)S(1)} %collective-permute-done, bf16[2048,192]{0,1:T(8,128)(2,1)} %bitcast.42), kind=kLoop, calls=%fused_computation.4 | loop fusion | flops 3145728 | bytes 3145728 | tf_op jit(solution)/shard_map/concatenate | solution.py:42
  29.8 0.0 all-gather.6.cloned.1.call-start
  29.8 1.8 %collective-permute-start.1 = (bf16[2048,192]{0,1:T(8,128)(2,1)S(1)}, bf16[2048,192]{0,1:T(8,128)(2,1)S(1)}, u32[]{:S(2)}, u32[]{:S(2)}) collective-permute-start(bf16[2048,192]{0,1:T(8,128)(2,1)S(1)} %bitcast.43), channel_id=1, source_target_pairs={{0,2},{2,0},{4,6},{6,4},{1,3},{3,1},{5,7},{7,5},{8,10},{10,8},{12,... | collective-permute-start | bytes 2359304 | tf_op jit(solution)/shard_map/ppermute | solution.py:8
  31.7 17.0 %collective-permute-done.1 = bf16[2048,192]{0,1:T(8,128)(2,1)S(1)} collective-permute-done((bf16[2048,192]{0,1:T(8,128)(2,1)S(1)}, bf16[2048,192]{0,1:T(8,128)(2,1)S(1)}, u32[]{:S(2)}, u32[]{:S(2)}) %collective-permute-start.1) | collective-permute-done | bytes 786464 | tf_op jit(solution)/shard_map/ppermute | solution.py:8
  48.6 1.3 pad_maximum_fusion.1
  49.9 0.0 all-gather.6.cloned.1.call-update
  49.9 0.0 all-gather.8.cloned.1.call-start
  50.0 1.5 %collective-permute-start.2 = (bf16[2048,192]{0,1:T(8,128)(2,1)S(1)}, bf16[2048,192]{0,1:T(8,128)(2,1)S(1)}, u32[]{:S(2)}, u32[]{:S(2)}) collective-permute-start(bf16[2048,192]{0,1:T(8,128)(2,1)S(1)} %bitcast.45), channel_id=1, source_target_pairs={{0,2},{2,0},{4,6},{6,4},{1,3},{3,1},{5,7},{7,5},{8,10},{10,8},{12,... | collective-permute-start | bytes 2359304 | tf_op jit(solution)/shard_map/ppermute | solution.py:8
  51.5 16.4 %collective-permute-done.2 = bf16[2048,192]{0,1:T(8,128)(2,1)S(1)} collective-permute-done((bf16[2048,192]{0,1:T(8,128)(2,1)S(1)}, bf16[2048,192]{0,1:T(8,128)(2,1)S(1)}, u32[]{:S(2)}, u32[]{:S(2)}) %collective-permute-start.2) | collective-permute-done | bytes 786464 | tf_op jit(solution)/shard_map/ppermute | solution.py:8
  67.9 1.3 pad_maximum_fusion.2
  69.2 0.0 all-gather.8.cloned.1.call-update
  69.2 0.1 copy.11
  69.3 0.1 eq.17
  69.5 0.1 copy.10
  69.6 0.1 mul.48
  69.7 0.1 fusion.4
  69.8 0.2 reduce_window_sum.11
  70.0 0.2 select_reduce_fusion
  70.2 3.2 %scatter_custom_fusion = bf16[192,2048]{1,0:T(8,128)(2,1)S(1)} fusion(s32[128]{0:T(128)S(1)} %fusion.8, bf16[64,2048]{1,0:T(8,128)(2,1)S(1)} %copy-done, s32[1024]{0:T(1024)S(1)} %pad_clamp_fusion.1, bf16[]{:T(256)} %constant.41.clone.1), kind=kCustom, calls=%fused_computation.9 | custom fusion | bytes 786434 | tf_op jit(solution)/shard_map/scatter | solution.py:36
  73.5 23.6 %all_to_all.10 = bf16[8,24,2048]{2,1,0:T(8,128)(2,1)S(1)} all-to-all(bf16[8,24,2048]{2,1,0:T(8,128)(2,1)S(1)} %bitcast.38), channel_id=1, replica_groups=mesh['parts'=2,'group'=2,'dev'=4,'pair'=2] {'group','dev'}, dimensions={0} | all-to-all | bytes 1572864 | tf_op jit(solution)/shard_map/all_to_all | solution.py:39
  97.1 3.1 %fusion.12 = f32[192,768]{1,0:T(8,128)S(1)} fusion(bf16[192,2048]{1,0:T(8,128)(2,1)S(1)} %bitcast.39, bf16[2048,768]{0,1:T(8,128)(2,1)} %all-gather.4.cloned.1.call-done), kind=kOutput, calls=%fused_computation.34 | convolution fusion | flops 603979776 | bytes 4521984 | tf_op jit(solution)/shard_map/dot_general | solution.py:12
  100.2 0.0 all-gather.6.cloned.1.call-done
  100.2 0.0 all-gather.8.cloned.1.call-done
  100.3 6.0 %convolution_convert_fusion = bf16[192,2048]{1,0:T(8,128)(2,1)} fusion(bf16[2048,768]{0,1:T(8,128)(2,1)} %all-gather.8.cloned.1.call-done, f32[192,768]{1,0:T(8,128)S(1)} %fusion.12, bf16[192,2048]{1,0:T(8,128)(2,1)S(1)} %bitcast.40, bf16[2048,768]{0,1:T(8,128)(2,1)} %all-gather.6.cloned.1.call-done), kind=kOutput, calls=%fused_computation.3 | convolution fusion | flops 1209237504 | bytes 8454144 | tf_op jit(solution)/shard_map/dot_general | solution.py:15
  106.3 3.5 %all-to-all-start.1 = ((bf16[8,24,2048]{2,1,0:T(8,128)(2,1)}), bf16[8,24,2048]{2,1,0:T(8,128)(2,1)S(1)}, u32[]{:S(2)}, u32[]{:S(2)}) async-start(bf16[8,24,2048]{2,1,0:T(8,128)(2,1)} %bitcast.10), calls=%async_computation.1 | async-start | bytes 1572864 | tf_op jit(solution)/shard_map/all_to_all | solution.py:52
  109.9 0.1 copy.12
  110.0 18.6 %all-to-all-done.1 = bf16[8,24,2048]{2,1,0:T(8,128)(2,1)S(1)} async-done(((bf16[8,24,2048]{2,1,0:T(8,128)(2,1)}), bf16[8,24,2048]{2,1,0:T(8,128)(2,1)S(1)}, u32[]{:S(2)}, u32[]{:S(2)}) %all-to-all-start.1) | async-done | bytes 786464 | tf_op jit(solution)/shard_map/all_to_all | solution.py:52
  128.6 0.9 gather_fusion
  129.5 0.7 reshape.149
  130.2 2.3 %multiply_reduce_fusion = bf16[64,2048]{1,0:T(8,128)(2,1)} fusion(f32[64,2,2048]{2,1,0:T(2,128)S(1)} %reshape.149, f32[64,2]{1,0:T(8,128)S(1)} %copy.12), kind=kLoop, calls=%fused_computation.7 | loop fusion | flops 393216 | bytes 1311232 | tf_op jit(solution)/shard_map/reduce_sum | solution.py:55
  (20 shorter events, 0.1 us)
Async XLA Ops:
  6.5 63.7 %copy-start = (bf16[64,2048]{1,0:T(8,128)(2,1)S(1)}, bf16[64,2048]{1,0:T(8,128)(2,1)}, u32[]{:S(2)}) copy-start(bf16[64,2048]{1,0:T(8,128)(2,1)} %param.6) | copy-start | bytes 786436
  6.5 23.3 %copy-start.1 = (bf16[1,2048,192]{1,2,0:T(8,128)(2,1)S(1)}, bf16[1,2048,192]{1,2,0:T(8,128)(2,1)}, u32[]{:S(2)}) copy-start(bf16[1,2048,192]{1,2,0:T(8,128)(2,1)} %param.10) | copy-start | bytes 2359300
  6.5 90.6 %all-gather.4.cloned.1.call-start = ((), (), s32[]{:S(2)}) async-start(), calls=%async_computation.2 | async-start | bytes 4718592 | tf_op jit(solution)/shard_map/all_gather | solution.py:46
  6.5 20.8 %collective-permute-start = (bf16[2048,192]{0,1:T(8,128)(2,1)}, bf16[2048,192]{0,1:T(8,128)(2,1)S(1)}, u32[]{:S(2)}, u32[]{:S(2)}) collective-permute-start(bf16[2048,192]{0,1:T(8,128)(2,1)} %bitcast.41), channel_id=1, source_target_pairs={{0,2},{2,0},{4,6},{6,4},{1,3},{3,1},{5,7},{7,5},{8,10},{10,8},{12,... | collective-permute-start | bytes 2359304 | tf_op jit(solution)/shard_map/ppermute | solution.py:8
  29.8 20.2 %copy-start.2 = (bf16[1,2048,192]{1,2,0:T(8,128)(2,1)S(1)}, bf16[1,2048,192]{1,2,0:T(8,128)(2,1)}, u32[]{:S(2)}) copy-start(bf16[1,2048,192]{1,2,0:T(8,128)(2,1)} %param.11) | copy-start | bytes 2359300
  29.8 70.4 %all-gather.6.cloned.1.call-start = ((), (), s32[]{:S(2)}) async-start(), calls=%async_computation.3 | async-start | bytes 4718592 | tf_op jit(solution)/shard_map/all_gather | solution.py:47
  29.8 18.8 %collective-permute-start.1 = (bf16[2048,192]{0,1:T(8,128)(2,1)S(1)}, bf16[2048,192]{0,1:T(8,128)(2,1)S(1)}, u32[]{:S(2)}, u32[]{:S(2)}) collective-permute-start(bf16[2048,192]{0,1:T(8,128)(2,1)S(1)} %bitcast.43), channel_id=1, source_target_pairs={{0,2},{2,0},{4,6},{6,4},{1,3},{3,1},{5,7},{7,5},{8,10},{10,8},{12,... | collective-permute-start | bytes 2359304 | tf_op jit(solution)/shard_map/ppermute | solution.py:8
  49.9 19.3 %copy-start.3 = (s32[64,2]{0,1:T(2,128)S(1)}, s32[64,2]{0,1:T(2,128)}, u32[]{:S(2)}) copy-start(s32[64,2]{0,1:T(2,128)} %param.7) | copy-start | bytes 1540
  49.9 50.3 %all-gather.8.cloned.1.call-start = ((), (), s32[]{:S(2)}) async-start(), calls=%async_computation.4 | async-start | bytes 4718592 | tf_op jit(solution)/shard_map/all_gather | solution.py:48
  50.0 17.9 %collective-permute-start.2 = (bf16[2048,192]{0,1:T(8,128)(2,1)S(1)}, bf16[2048,192]{0,1:T(8,128)(2,1)S(1)}, u32[]{:S(2)}, u32[]{:S(2)}) collective-permute-start(bf16[2048,192]{0,1:T(8,128)(2,1)S(1)} %bitcast.45), channel_id=1, source_target_pairs={{0,2},{2,0},{4,6},{6,4},{1,3},{3,1},{5,7},{7,5},{8,10},{10,8},{12,... | collective-permute-start | bytes 2359304 | tf_op jit(solution)/shard_map/ppermute | solution.py:8
  100.2 9.6 %copy-start.4 = (f32[64,2]{0,1:T(2,128)S(1)}, f32[64,2]{0,1:T(2,128)}, u32[]{:S(2)}) copy-start(f32[64,2]{0,1:T(2,128)} %param.8) | copy-start | bytes 1540
  106.3 22.3 %all-to-all-start.1 = ((bf16[8,24,2048]{2,1,0:T(8,128)(2,1)}), bf16[8,24,2048]{2,1,0:T(8,128)(2,1)S(1)}, u32[]{:S(2)}, u32[]{:S(2)}) async-start(bf16[8,24,2048]{2,1,0:T(8,128)(2,1)} %bitcast.10), calls=%async_computation.1 | async-start | bytes 1572864 | tf_op jit(solution)/shard_map/all_to_all | solution.py:52
Sparse Core Ops, SparseCore 0:
  29.9 13.5 all-gather.3
  50.0 13.2 all-gather.5
  69.3 12.9 all-gather.7
where the time goes:
time: 139 us
  waiting for transfers between devices  69.8 us (50%)
  blocking collectives  23.6 us (17%)
  between operations  13.2 us (9%)
  starting transfers between devices  10 us (7%)
  matrix products  9.09 us (7%)
  other arithmetic  7.74 us (6%)
  local copies, waits for them, and re-layouts  5.42 us (4%)
    ppermute x3, waiting for transfers between devices, partner_2(): lax.ppermute(x, axis, [(i, i ^ 1 << apart) for i in range(lax.axis_size(a...  51.1 us
    all_to_all x1, blocking collectives, shards(): lax.all_to_all(outgoing, ('group', 'dev'), split_axis=0, concat_axis=0, t...  23.6 us
    all_to_all x1, waiting for transfers between devices, shards(): lax.all_to_all(answer, ('group', 'dev'), split_axis=0, concat_axis=0, til...  18.6 us
    ppermute x3, starting transfers between devices, partner_2(): lax.ppermute(x, axis, [(i, i ^ 1 << apart) for i in range(lax.axis_size(a...  6.39 us
    dot_general x1, matrix products, expert_block(): lax.dot_general(hidden, down_piece, (((1,), (1,)), ((), ())), preferred_e...  6.01 us
    all_to_all x1, starting transfers between devices, shards(): lax.all_to_all(answer, ('group', 'dev'), split_axis=0, concat_axis=0, til...  3.55 us
    scatter x1, local copies, waits for them, and re-layouts, shards(): jnp.zeros((dest_count * half_cap, features), jnp.bfloat16).at[position]  3.25 us
    dot_general x1, matrix products, expert_block(): jnp.dot(batch_rows, gate_piece, preferred_element_type=jnp.float32)  3.08 us
  transfers between devices with their start and end apart: 7, of which 4 were waited for; matrix products, arithmetic and copies ran while one was open for 7% of the time, Pallas kernels for 0%

commit v1 on v0

--- a/solution.py
+++ b/solution.py
@@ -1,7 +1,274 @@
+import functools
 import jax
 import jax.numpy as jnp
 from jax import lax
+from jax.experimental import pallas as pl
+from jax.experimental.pallas import tpu as pltpu
 from jax.sharding import PartitionSpec as P
+
+MESH = pl.DeviceIdType.MESH
+
+
+def fused(n, rows, early, ag_cuts, rs_cuts, tokens, table, gate, up, down, out, tok, tab, wg, wu, wd, part,
+          stage_z, land_z, stage_x, land_x, load_sem, swap_send, swap_recv, tab_send, tab_recv,
+          za_send, za_recv, xa_send, xa_recv, zr_send, zr_recv, xr_send, xr_recv):
+    g, d, p = lax.axis_index("group"), lax.axis_index("dev"), lax.axis_index("pair")
+    late = rows - early
+    wide = rows + early
+    features = tok.shape[2]
+
+    def remote(source, target, send, recv, where):
+        return pltpu.make_async_remote_copy(source, target, send, recv, device_id=where, device_id_type=MESH)
+
+    other_g, other_p = {"group": 1 - g}, {"pair": 1 - p}
+
+    own_load = pltpu.make_async_copy(tokens, tok.at[d, pl.ds(0, rows)], load_sem.at[0])
+    own_load.start()
+    loads = [
+        pltpu.make_async_copy(piece.at[0], full.at[0], load_sem.at[1 + i])
+        for i, (piece, full) in enumerate(((gate, wg), (up, wu), (down, wd)))
+    ]
+    for load in loads:
+        load.start()
+    tab[0, d] = table[...]
+
+    barrier = pltpu.get_barrier_semaphore()
+    plane = []
+    for off in range(1, 2 * n):
+        there = lax.rem(g * n + d + off, 2 * n)
+        plane.append((there // n, lax.rem(there, n)))
+    pl.semaphore_signal(barrier, inc=1, device_id=other_p, device_id_type=MESH)
+    for tg, td in plane:
+        pl.semaphore_signal(barrier, inc=1, device_id={"group": tg, "dev": td}, device_id_type=MESH)
+    pl.semaphore_wait(barrier, 2 * n)
+    own_load.wait()
+
+    def ag_z(src, side, k):
+        lo, size = ag_cuts[k]
+        block = tok.at[src, pl.ds(lo, size)]
+        return remote(block, block, za_send.at[side, src, k], za_recv.at[src, k], {"dev": d + 1 - 2 * side})
+
+    def has_next(side):
+        return d < n - 1 if side == 0 else d > 0
+
+    def ag_x(src, which):
+        lo, size = ((0, early), (early, late))[which]
+        return remote(tok.at[src, pl.ds(lo, size)], tok.at[src, pl.ds(rows + lo, size)],
+                      xa_send.at[src, which], xa_recv.at[src, which], other_g)
+
+    def rs_x(src):
+        return remote(stage_x.at[src, pl.ds(early, late)], land_x.at[src, pl.ds(early, late)],
+                      xr_send.at[src, 0], xr_recv.at[src, 0], other_g)
+
+    def rs_xa():
+        return remote(stage_x.at[d, pl.ds(0, early)], land_x.at[d, pl.ds(0, early)],
+                      xr_send.at[d, 1], xr_recv.at[d, 1], other_g)
+
+    def rs_z(src, side, k):
+        lo, size = rs_cuts[k]
+        return remote(stage_z.at[src, pl.ds(lo, size)], land_z.at[side, src, pl.ds(lo, size)],
+                      zr_send.at[src, k], zr_recv.at[side, src, k], {"dev": d + 1 - 2 * side})
+
+    def tab_copy(i):
+        tg, td = plane[i]
+        rel = jnp.where(tg == g, 0, 1)
+        return remote(tab.at[0, d], tab.at[rel, d], tab_send.at[i], tab_recv.at[rel, d], {"group": tg, "dev": td})
+
+    def tab_wait(i):
+        tg, td = plane[i]
+        rel = jnp.where(tg == g, 0, 1)
+        remote(tab.at[rel, td], tab.at[rel, td], tab_send.at[i], tab_recv.at[rel, td], other_g).wait_recv()
+
+    swaps = [
+        remote(piece.at[0], full.at[1], swap_send.at[i], swap_recv.at[i], other_p)
+        for i, (piece, full) in enumerate(((gate, wg), (up, wu), (down, wd)))
+    ]
+
+    own_cuts = [k for k, (lo, size) in enumerate(ag_cuts) if lo < rows]
+    far_cuts = [k for k, (lo, size) in enumerate(ag_cuts) if lo >= rows]
+    ag_x(d, 0).start()
+    for k in own_cuts:
+        for side in (0, 1):
+            pl.when(has_next(side))(lambda side=side, k=k: ag_z(d, side, k).start())
+    ag_x(d, 1).start()
+    for i in range(2 * n - 1):
+        tab_copy(i).start()
+    for swap in swaps:
+        swap.start()
+    ag_x(d, 0).wait_recv()
+    for k in far_cuts:
+        for side in (0, 1):
+            pl.when(has_next(side))(lambda side=side, k=k: ag_z(d, side, k).start())
+    for i in range(2 * n - 1):
+        tab_wait(i)
+    for load in loads:
+        load.wait()
+    for swap in swaps:
+        swap.wait_recv()
+
+    expert = (g * n + d) // 2
+    eye = lax.broadcasted_iota(jnp.int32, (rows, rows), 0) == lax.broadcasted_iota(jnp.int32, (rows, rows), 1)
+
+    def column(rel, src):
+        row = tab[rel, src, pl.ds(expert, 1), :]
+        return jnp.sum(jnp.where(eye, jnp.broadcast_to(row, (rows, rows)), 0.0), axis=1, keepdims=True)
+
+    tile = 512 if features % 512 == 0 else features
+
+    def compute(src):
+        x = tok[src]
+        scale = jnp.concatenate([column(0, src), column(1, src)], axis=0)
+        hidden = []
+        for j in range(2):
+            gate_act = jnp.dot(x, wg[j], preferred_element_type=jnp.float32)
+            up_act = jnp.dot(x, wu[j], preferred_element_type=jnp.float32)
+            hidden.append((gate_act / (1.0 + jnp.exp(-gate_act)) * up_act).astype(jnp.bfloat16))
+        for at in range(0, features, tile):
+            total = None
+            for j in range(2):
+                term = lax.dot_general(hidden[j], wd[j, at:at + tile, :], (((1,), (1,)), ((), ())),
+                                       preferred_element_type=jnp.float32)
+                total = term if total is None else total + term
+            total = total * scale
+            part[src, :, at:at + tile] = total[:wide]
+            stage_x[src, early:rows, at:at + tile] = total[wide:].astype(jnp.bfloat16)
+        rs_x(src).start()
+
+    def add_x(src):
+        rs_x(src).wait_recv()
+        part[src, early:rows] += land_x[src, early:rows].astype(jnp.float32)
+
+    def send_on(src, side, landed):
+        add_x(src)
+        for k, (lo, size) in enumerate(rs_cuts):
+            value = part[src, lo:lo + size]
+            if landed:
+                rs_z(src, side, k).wait_recv()
+                value = value + land_z[side, src, lo:lo + size].astype(jnp.float32)
+            stage_z[src, lo:lo + size] = value.astype(jnp.bfloat16)
+            rs_z(src, side, k).start()
+
+    def step(s, carry):
+        for side in (0, 1):
+            src = d - s if side == 0 else d + s
+            valid = jnp.logical_and(s >= 1, jnp.logical_and(src >= 0, src < n))
+
+            @pl.when(valid)
+            def _():
+                for k in range(len(ag_cuts)):
+                    ag_z(src, side, k).wait_recv()
+                    pl.when(has_next(side))(lambda: ag_z(src, side, k).start())
+                    if k == own_cuts[-1]:
+                        ag_x(src, 1).start()
+
+        def one(side, carry):
+            b = s - 1
+            src = d - b + 2 * b * side
+            valid = jnp.logical_and(jnp.logical_and(b >= 0, jnp.logical_or(side == 0, b >= 1)), jnp.logical_and(src >= 0, src < n))
+
+            @pl.when(valid)
+            def _():
+                ag_x(src, 1).wait_recv()
+                compute(src)
+            return carry
+
+        lax.fori_loop(0, 2, one, 0)
+
+        for side in (0, 1):
+            c = s - 2
+            src = d + c if side == 0 else d - c
+            end = d == 0 if side == 0 else d == n - 1
+            valid = jnp.logical_and(jnp.logical_and(c >= 1, end), jnp.logical_and(src >= 0, src < n))
+            pl.when(valid)(lambda: send_on(src, side, False))
+        return carry
+
+    lax.fori_loop(0, n + 2, step, 0)
+
+    def relay(t, carry):
+        for side in (0, 1):
+            src = t if side == 0 else n - 1 - t
+            valid = jnp.logical_and(d > 0, d < src) if side == 0 else jnp.logical_and(d < n - 1, d > src)
+            pl.when(valid)(lambda: send_on(src, side, True))
+        return carry
+
+    lax.fori_loop(1, n, relay, 0)
+
+    add_x(d)
+    for k, (lo, size) in enumerate(rs_cuts):
+        for side in (0, 1):
+            @pl.when(d > 0 if side == 0 else d < n - 1)
+            def _():
+                rs_z(d, side, k).wait_recv()
+                part[d, lo:lo + size] += land_z[side, d, lo:lo + size].astype(jnp.float32)
+        if lo <= rows < lo + size:
+            stage_x[d, 0:early] = part[d, rows:wide].astype(jnp.bfloat16)
+            rs_xa().start()
+    out[early:rows] = part[d, early:rows].astype(jnp.bfloat16)
+    rs_xa().wait_recv()
+    out[0:early] = (part[d, 0:early] + land_x[d, 0:early].astype(jnp.float32)).astype(jnp.bfloat16)
+
+    for swap in swaps:
+        swap.wait_send()
+    for i in range(2 * n - 1):
+        tab_copy(i).wait_send()
+    ag_x(d, 0).wait_send()
+    rs_xa().wait_send()
+
+    def drain(src, carry):
+        ag_x(src, 1).wait_send()
+        rs_x(src).wait_send()
+        for side in (0, 1):
+            @pl.when(jnp.logical_and(has_next(side), src <= d if side == 0 else src >= d))
+            def _():
+                for k in range(len(ag_cuts)):
+                    ag_z(src, side, k).wait_send()
+
+            @pl.when(src > d if side == 0 else src < d)
+            def _():
+                for k in range(len(rs_cuts)):
+                    rs_z(src, side, k).wait_send()
+        return carry
+
+    lax.fori_loop(0, n, drain, 0)
+
+
+def near(tokens, expert_ids, route_scores, w_gate, w_up, w_down):
+    rows, features = tokens.shape
+    n = lax.axis_size("dev")
+    experts = n
+    units = w_gate.shape[2]
+    early = rows // 4
+    half = rows // 2
+    ag_cuts = ((0, half), (half, half), (rows, early))
+    rs_cuts = ((rows, early), (0, half), (half, half))
+    route_weight = route_scores / jnp.sum(route_scores, axis=1, keepdims=True)
+    names = jnp.arange(experts, dtype=jnp.int32)[:, None, None]
+    table = jnp.sum(jnp.where(expert_ids[None] == names, route_weight[None], 0.0), axis=2)
+    wide = rows + early
+    dma, bf16, f32 = pltpu.SemaphoreType.DMA, jnp.bfloat16, jnp.float32
+    vmem, hbm = pl.BlockSpec(memory_space=pltpu.VMEM), pl.BlockSpec(memory_space=pl.ANY)
+    return pl.pallas_call(
+        functools.partial(fused, n, rows, early, ag_cuts, rs_cuts),
+        out_shape=jax.ShapeDtypeStruct((rows, features), bf16),
+        in_specs=[hbm, vmem, hbm, hbm, hbm],
+        out_specs=vmem,
+        scratch_shapes=[
+            pltpu.VMEM((n, 2 * rows, features), bf16),
+            pltpu.VMEM((2, n, experts, rows), f32),
+            pltpu.VMEM((2, features, units), bf16),
+            pltpu.VMEM((2, features, units), bf16),
+            pltpu.VMEM((2, features, units), bf16),
+            pltpu.VMEM((n, wide, features), f32),
+            pltpu.VMEM((n, wide, features), bf16),
+            pltpu.VMEM((2, n, wide, features), bf16),
+            pltpu.VMEM((n, rows, features), bf16),
+            pltpu.VMEM((n, rows, features), bf16),
+            dma((4,)), dma((3,)), dma((3,)), dma((2 * n - 1,)), dma((2, n)),
+            dma((2, n, len(ag_cuts))), dma((n, len(ag_cuts))), dma((n, 2)), dma((n, 2)),
+            dma((n, len(rs_cuts))), dma((2, n, len(rs_cuts))), dma((n, 2)), dma((n, 2)),
+        ],
+        compiler_params=pltpu.CompilerParams(collective_id=0, has_side_effects=True, vmem_limit_bytes=56 * 2**20),
+    )(tokens, table, w_gate, w_up, w_down)
 
 
 def partner_2(x, axis, apart):
@@ -66,4 +333,5 @@
         P(("group", "dev"), None, "pair"),
     )
     out_specs = P(("parts", "group", "dev", "pair"), None)
-    return jax.shard_map(shards, mesh=mesh, in_specs=in_specs, out_specs=out_specs, check_vma=False)
+    few = mesh.shape["group"] == 2 and mesh.shape["pair"] == 2 and mesh.shape["dev"] <= 4
+    return jax.shard_map(near if few else shards, mesh=mesh, in_specs=in_specs, out_specs=out_specs, check_vma=False)

time: 139 us -> 80.4 us (0.58)
  Pallas kernels: 0 us -> 71.5 us
  waiting for transfers between devices: 69.8 us -> 0 us
  blocking collectives: 23.6 us -> 0 us
  between operations: 13.2 us -> 0.03 us
  starting transfers between devices: 10 us -> 0 us
  matrix products: 9.09 us -> 0 us
  other arithmetic: 7.74 us -> 1.36 us
  local copies, waits for them, and re-layouts: 5.42 us -> 7.26 us
    pallas_call x0 -> x1, Pallas kernels: none -> 71.5 us  [near(): pl.pallas_call(functools.partial(fused, n, rows, early, ag_cuts, rs_cuts)...]
    ppermute x3 -> x0, waiting for transfers between devices: 51.1 us -> none  [partner_2(): lax.ppermute(x, axis, [(i, i ^ 1 << apart) for i in range(lax.axis_size(a...]
    all_to_all x1 -> x0, blocking collectives: 23.6 us -> none  [shards(): lax.all_to_all(outgoing, ('group', 'dev'), split_axis=0, concat_axis=0, t...]
    all_to_all x1 -> x0, waiting for transfers between devices: 18.6 us -> none  [shards(): lax.all_to_all(answer, ('group', 'dev'), split_axis=0, concat_axis=0, til...]
    dot_general x2 -> x0, matrix products: 9.09 us -> none  [the longest x1 6.01 us: expert_block(): lax.dot_general(hidden, down_piece, (((1,), (1,)), ((), ())), preferred_e...]
    unnamed x11 -> x12, local copies, waits for them, and re-layouts: 0.12 us -> 7.26 us
    ppermute x3 -> x0, starting transfers between devices: 6.39 us -> none  [partner_2(): lax.ppermute(x, axis, [(i, i ^ 1 << apart) for i in range(lax.axis_size(a...]
    concatenate x3 -> x0, other arithmetic: 4.97 us -> none  [the longest x1 2.42 us: shards(): gate_half = jnp.concatenate([w_gate[0], partner[0]], axis=1)]
  transfers between devices with their start and end apart: 7 -> 0, of which waited for: 4 -> 0; matrix products, arithmetic and copies ran while one was open for 7% -> 0% of each run, Pallas kernels for 0% -> 0%
where the time goes in v1:
time: 80.4 us; the launch traced here: 80.1 us
  Pallas kernels  71.5 us (89%)
  local copies, waits for them, and re-layouts  7.26 us (9%)
  other arithmetic  1.36 us (2%)
    pallas_call x1, Pallas kernels, near(): pl.pallas_call(functools.partial(fused, n, rows, early, ag_cuts, rs_cuts)...  71.5 us
    unnamed x12, local copies, waits for them, and re-layouts  7.26 us

profile of v1, /device:TPU:0, one launch (start us, length us, event | category | flops | bytes accessed | tf_op | source)
XLA Modules:
  0.0 80.1 jit_solution(1174779677944370370)
XLA Ops:
  0.0 0.0 copy-start.2
  0.0 0.8 reduce_sum.18
  0.8 0.0 copy-done.2
  0.8 0.0 copy-start.3
  0.8 0.7 copy-done.3
  1.5 0.6 select_reduce_fusion.table
  2.0 0.0 copy-start
  2.0 2.3 %copy.12.gate = bf16[1,2048,192]{2,1,0:T(8,128)(2,1)} copy(bf16[1,2048,192]{1,2,0:T(8,128)(2,1)} %param.9) | data formatting | bytes 1572864 | tf_op args[3]
  4.3 0.0 copy-done
  4.4 0.0 copy-start.1
  4.4 1.3 %copy.13.up = bf16[1,2048,192]{2,1,0:T(8,128)(2,1)} copy(bf16[1,2048,192]{1,2,0:T(8,128)(2,1)S(1)} %copy-done) | data formatting | bytes 1572864 | tf_op args[4]
  5.7 0.0 copy-done.1
  5.7 1.3 %copy.14.down = bf16[1,2048,192]{2,1,0:T(8,128)(2,1)} copy(bf16[1,2048,192]{1,2,0:T(8,128)(2,1)S(1)} %copy-done.1) | data formatting | bytes 1572864 | tf_op args[5]
  7.0 71.5 %shard_map.64 = bf16[64,2048]{1,0:T(8,128)(2,1)} custom-call(bf16[64,2048]{1,0:T(8,128)(2,1)} %tokens.1, f32[4,64]{1,0:T(4,128)} %select_reduce_fusion.table, bf16[1,2048,192]{2,1,0:T(8,128)(2,1)} %copy.12.gate, bf16[1,2048,192]{2,1,0:T(8,128)(2,1)} %copy.13.up, bf16[1,2048,192]{2,1,0:T(8,128)(2,1)} %copy.14.down), custom_call_target="tpu_custom_call" | custom-call | tf_op jit(solution)/shard_map/pallas_call | solution.py:250
  78.5 1.7 %copy.16 = bf16[64,2048]{1,0:T(8,128)(2,1)} copy(bf16[64,2048]{1,0:T(8,128)(2,1)} %shard_map.64) | data formatting | bytes 524288
  (1 shorter events, 0.0 us)
Async XLA Ops:
  0.0 0.8 copy-start.2
  0.8 0.7 copy-start.3
  2.0 2.3 %copy-start = (bf16[1,2048,192]{1,2,0:T(8,128)(2,1)S(1)}, bf16[1,2048,192]{1,2,0:T(8,128)(2,1)}, u32[]{:S(2)}) copy-start(bf16[1,2048,192]{1,2,0:T(8,128)(2,1)} %param.10) | copy-start | bytes 2359300
  4.4 1.3 %copy-start.1 = (bf16[1,2048,192]{1,2,0:T(8,128)(2,1)S(1)}, bf16[1,2048,192]{1,2,0:T(8,128)(2,1)}, u32[]{:S(2)}) copy-start(bf16[1,2048,192]{1,2,0:T(8,128)(2,1)} %param.11) | copy-start | bytes 2359300

commit v2 on v1

v2 whole, which is shorter than its diff:
```python
import functools
import jax
import jax.numpy as jnp
from jax import lax
from jax.experimental import pallas as pl
from jax.experimental.pallas import tpu as pltpu
from jax.sharding import PartitionSpec as P

MESH = pl.DeviceIdType.MESH


def fused(n, rows, early, ag_cuts, rs_cuts, tokens, ids, scores, gate, up, down, out, tok, tab, wg, wu, wd, part,
          stage_z, land_z, stage_x, land_x, load_sem, swap_send, swap_recv, tab_send, tab_recv,
          za_send, za_recv, xa_send, xa_recv, zr_send, zr_recv, xr_send, xr_recv):
    g, d, p = lax.axis_index("group"), lax.axis_index("dev"), lax.axis_index("pair")
    x_cuts = [(0, early)]
    x_of = {}
    for k, (lo, size) in enumerate(ag_cuts):
        if lo < rows and lo + size > early:
            x_of[k] = len(x_cuts)
            x_cuts.append((max(lo, early), lo + size - max(lo, early)))
    rest = range(1, len(x_cuts))
    wide = rows + early
    features = tok.shape[2]
    units = gate.shape[1]

    def remote(source, target, send, recv, where):
        return pltpu.make_async_remote_copy(source, target, send, recv, device_id=where, device_id_type=MESH)

    other_g, other_p = {"group": 1 - g}, {"pair": 1 - p}

    own_load = pltpu.make_async_copy(tokens, tok.at[d, pl.ds(0, rows)], load_sem.at[0])
    own_load.start()
    loads = [
        pltpu.make_async_copy(piece.at[0], full.at[pl.ds(0, units)], load_sem.at[1 + i])
        for i, (piece, full) in enumerate(((gate, wg), (up, wu), (down, wd)))
    ]
    for load in loads:
        load.start()
    route_weight = scores[...] / jnp.sum(scores[...], axis=0, keepdims=True)
    experts = tab.shape[2]
    names = lax.broadcasted_iota(jnp.int32, (experts, rows), 0)
    table = jnp.zeros((experts, rows), jnp.float32)
    for k in range(ids.shape[0]):
        table += jnp.where(ids[k:k + 1] == names, route_weight[k:k + 1], 0.0)
    tab[d, 0] = table

    barrier = pltpu.get_barrier_semaphore()
    pl.semaphore_signal(barrier, inc=1, device_id=other_p, device_id_type=MESH)
    pl.semaphore_signal(barrier, inc=1, device_id=other_g, device_id_type=MESH)
    for side in (0, 1):
        @pl.when(d < n - 1 if side == 0 else d > 0)
        def _():
            pl.semaphore_signal(barrier, inc=1, device_id={"dev": d + 1 - 2 * side}, device_id_type=MESH)
    inner = jnp.logical_and(d > 0, d < n - 1)

    @pl.when(inner)
    def _():
        pl.semaphore_wait(barrier, 4)

    @pl.when(jnp.logical_not(inner))
    def _():
        pl.semaphore_wait(barrier, 3)
    own_load.wait()

    def ag_z(src, side, k):
        lo, size = ag_cuts[k]
        block = tok.at[src, pl.ds(lo, size)]
        return remote(block, block, za_send.at[side, src, k], za_recv.at[src, k], {"dev": d + 1 - 2 * side})

    def has_next(side):
        return d < n - 1 if side == 0 else d > 0

    def ag_x(src, which):
        lo, size = x_cuts[which]
        return remote(tok.at[src, pl.ds(lo, size)], tok.at[src, pl.ds(rows + lo, size)],
                      xa_send.at[src, which], xa_recv.at[src, which], other_g)

    def rs_x(src, which):
        block = pl.ds(*x_cuts[which])
        return remote(stage_x.at[src, block], land_x.at[src, block],
                      xr_send.at[src, which], xr_recv.at[src, which], other_g)

    def rs_z(src, side, k):
        lo, size = rs_cuts[k]
        return remote(stage_z.at[src, pl.ds(lo, size)], land_z.at[side, src, pl.ds(lo, size)],
                      zr_send.at[src, k], zr_recv.at[side, src, k], {"dev": d + 1 - 2 * side})

    def tab_x():
        return remote(tab.at[d, 0], tab.at[d, 1], tab_send.at[2 * n], tab_recv.at[n], other_g)

    def tab_z(src, side):
        return remote(tab.at[src], tab.at[src], tab_send.at[side * n + src], tab_recv.at[src], {"dev": d + 1 - 2 * side})

    swaps = [
        remote(piece.at[0], full.at[pl.ds(units, units)], swap_send.at[i], swap_recv.at[i], other_p)
        for i, (piece, full) in enumerate(((gate, wg), (up, wu), (down, wd)))
    ]

    own_cuts = [k for k, (lo, size) in enumerate(ag_cuts) if lo < rows]
    far_cuts = [k for k, (lo, size) in enumerate(ag_cuts) if lo >= rows]
    tab_x().start()
    ag_x(d, 0).start()
    for k in own_cuts:
        for side in (0, 1):
            pl.when(has_next(side))(lambda side=side, k=k: ag_z(d, side, k).start())
    for which in rest:
        ag_x(d, which).start()
    for swap in swaps:
        swap.start()
    tab_x().wait_recv()
    for side in (0, 1):
        pl.when(has_next(side))(lambda side=side: tab_z(d, side).start())
    ag_x(d, 0).wait_recv()
    for k in far_cuts:
        for side in (0, 1):
            pl.when(has_next(side))(lambda side=side, k=k: ag_z(d, side, k).start())
    expert = (g * n + d) // 2
    eye = lax.broadcasted_iota(jnp.int32, (rows, rows), 0) == lax.broadcasted_iota(jnp.int32, (rows, rows), 1)

    def column(rel, src):
        row = tab[src, rel, pl.ds(expert, 1), :]
        return jnp.sum(jnp.where(eye, jnp.broadcast_to(row, (rows, rows)), 0.0), axis=1, keepdims=True)

    tile = 512 if features % 512 == 0 else features

    def compute(src):
        x = tok[src]
        scale = jnp.concatenate([column(0, src), column(1, src)], axis=0)
        over_features = (((1,), (1,)), ((), ()))
        gate_act = lax.dot_general(x, wg[...], over_features, preferred_element_type=jnp.float32)
        up_act = lax.dot_general(x, wu[...], over_features, preferred_element_type=jnp.float32)
        hidden = (gate_act / (1.0 + jnp.exp(-gate_act)) * up_act).astype(jnp.bfloat16)
        for at in range(0, features, tile):
            total = scale * jnp.dot(hidden, wd[:, at:at + tile], preferred_element_type=jnp.float32)
            part[src, :, at:at + tile] = total[:wide]
            stage_x[src, early:rows, at:at + tile] = total[wide:].astype(jnp.bfloat16)
        for which in rest:
            rs_x(src, which).start()

    rs_x_of = {k: x_of[ag_cuts.index(cut)] for k, cut in enumerate(rs_cuts) if ag_cuts.index(cut) in x_of}

    def add_x(src, k):
        if k in rs_x_of:
            lo, size = x_cuts[rs_x_of[k]]
            rs_x(src, rs_x_of[k]).wait_recv()
            part[src, lo:lo + size] += land_x[src, lo:lo + size].astype(jnp.float32)

    def send_on(src, side, landed):
        for k, (lo, size) in enumerate(rs_cuts):
            add_x(src, k)
            value = part[src, lo:lo + size]
            if landed:
                rs_z(src, side, k).wait_recv()
                value = value + land_z[side, src, lo:lo + size].astype(jnp.float32)
            stage_z[src, lo:lo + size] = value.astype(jnp.bfloat16)
            rs_z(src, side, k).start()

    def step(s, carry):
        @pl.when(s == 1)
        def _():
            for load in loads:
                load.wait()
            for swap in swaps:
                swap.wait_recv()

        def one(side, carry):
            b = s - 1
            src = d - b + 2 * b * side
            valid = jnp.logical_and(jnp.logical_and(b >= 0, jnp.logical_or(side == 0, b >= 1)), jnp.logical_and(src >= 0, src < n))

            @pl.when(valid)
            def _():
                for which in rest:
                    ag_x(src, which).wait_recv()
                compute(src)
            return carry

        lax.fori_loop(0, 2, one, 0)

        for side in (0, 1):
            src = d - s if side == 0 else d + s
            valid = jnp.logical_and(s >= 1, jnp.logical_and(src >= 0, src < n))

            @pl.when(valid)
            def _():
                tab_z(src, side).wait_recv()
                pl.when(has_next(side))(lambda: tab_z(src, side).start())
                for k in range(len(ag_cuts)):
                    ag_z(src, side, k).wait_recv()
                    pl.when(has_next(side))(lambda: ag_z(src, side, k).start())
                    if k in x_of:
                        ag_x(src, x_of[k]).start()

        for side in (0, 1):
            c = s - 1
            src = d + c if side == 0 else d - c
            end = d == 0 if side == 0 else d == n - 1
            valid = jnp.logical_and(jnp.logical_and(c >= 1, end), jnp.logical_and(src >= 0, src < n))
            pl.when(valid)(lambda: send_on(src, side, False))
        return carry

    lax.fori_loop(0, n + 1, step, 0)

    def relay(t, carry):
        for side in (0, 1):
            src = t if side == 0 else n - 1 - t
            valid = jnp.logical_and(d > 0, d < src) if side == 0 else jnp.logical_and(d < n - 1, d > src)
            pl.when(valid)(lambda: send_on(src, side, True))
        return carry

    lax.fori_loop(1, n, relay, 0)

    for k, (lo, size) in enumerate(rs_cuts):
        add_x(d, k)
        for side in (0, 1):
            @pl.when(d > 0 if side == 0 else d < n - 1)
            def _():
                rs_z(d, side, k).wait_recv()
                part[d, lo:lo + size] += land_z[side, d, lo:lo + size].astype(jnp.float32)
        if lo + size == wide:
            stage_x[d, 0:early] = part[d, rows:wide].astype(jnp.bfloat16)
            rs_x(d, 0).start()
    out[early:rows] = part[d, early:rows].astype(jnp.bfloat16)
    rs_x(d, 0).wait_recv()
    out[0:early] = (part[d, 0:early] + land_x[d, 0:early].astype(jnp.float32)).astype(jnp.bfloat16)

    for swap in swaps:
        swap.wait_send()
    tab_x().wait_send()
    ag_x(d, 0).wait_send()
    rs_x(d, 0).wait_send()

    def drain(src, carry):
        for which in rest:
            ag_x(src, which).wait_send()
            rs_x(src, which).wait_send()
        for side in (0, 1):
            @pl.when(jnp.logical_and(has_next(side), src <= d if side == 0 else src >= d))
            def _():
                tab_z(src, side).wait_send()
                for k in range(len(ag_cuts)):
                    ag_z(src, side, k).wait_send()

            @pl.when(src > d if side == 0 else src < d)
            def _():
                for k in range(len(rs_cuts)):
                    rs_z(src, side, k).wait_send()
        return carry

    lax.fori_loop(0, n, drain, 0)


def near(tokens, expert_ids, route_scores, w_gate, w_up, w_down):
    rows, features = tokens.shape
    n = lax.axis_size("dev")
    experts = n
    units = w_gate.shape[2]
    early = rows // 2
    wide = rows + early
    fine = rows // 4
    ag_cuts = tuple((at, fine) for at in range(0, wide, fine))
    rs_cuts = tuple((at, fine) for at in range(rows, wide, fine)) + tuple((at, fine) for at in range(0, rows, fine))
    dma, bf16, f32 = pltpu.SemaphoreType.DMA, jnp.bfloat16, jnp.float32
    vmem, hbm = pl.BlockSpec(memory_space=pltpu.VMEM), pl.BlockSpec(memory_space=pl.ANY)
    return pl.pallas_call(
        functools.partial(fused, n, rows, early, ag_cuts, rs_cuts),
        out_shape=jax.ShapeDtypeStruct((rows, features), bf16),
        in_specs=[hbm, vmem, vmem, hbm, hbm, hbm],
        out_specs=vmem,
        scratch_shapes=[
            pltpu.VMEM((n, 2 * rows, features), bf16),
            pltpu.VMEM((n, 2, experts, rows), f32),
            pltpu.VMEM((2 * units, features), bf16),
            pltpu.VMEM((2 * units, features), bf16),
            pltpu.VMEM((2 * units, features), bf16),
            pltpu.VMEM((n, wide, features), f32),
            pltpu.VMEM((n, wide, features), bf16),
            pltpu.VMEM((2, n, wide, features), bf16),
            pltpu.VMEM((n, rows, features), bf16),
            pltpu.VMEM((n, rows, features), bf16),
            dma((4,)), dma((3,)), dma((3,)), dma((2 * n + 1,)), dma((n + 1,)),
            dma((2, n, len(ag_cuts))), dma((n, len(ag_cuts))), dma((n, len(ag_cuts))), dma((n, len(ag_cuts))),
            dma((n, len(rs_cuts))), dma((2, n, len(rs_cuts))), dma((n, len(ag_cuts))), dma((n, len(ag_cuts))),
        ],
        compiler_params=pltpu.CompilerParams(collective_id=0, has_side_effects=True, vmem_limit_bytes=56 * 2**20),
    )(tokens, expert_ids.T, route_scores.T, *(jnp.swapaxes(w, 1, 2) for w in (w_gate, w_up, w_down)))


def partner_2(x, axis, apart):
    return lax.ppermute(x, axis, [(i, i ^ 1 << apart) for i in range(lax.axis_size(axis))])


def expert_block(batch_rows, gate_piece, up_piece, down_piece):
    gate_act = jnp.dot(batch_rows, gate_piece, preferred_element_type=jnp.float32)
    up_act = jnp.dot(batch_rows, up_piece, preferred_element_type=jnp.float32)
    hidden = (jax.nn.silu(gate_act) * up_act).astype(jnp.bfloat16)
    return lax.dot_general(
        hidden, down_piece, (((1,), (1,)), ((), ())), preferred_element_type=jnp.float32
    )


def shards(tokens, expert_ids, route_scores, w_gate, w_up, w_down):
    rows_dev, features = tokens.shape
    top_count = expert_ids.shape[1]
    dest_count = lax.axis_size(("group", "dev"))
    experts = dest_count // 2
    capacity = 2 * max(1, 3 * rows_dev * top_count // (4 * experts))
    half_cap = capacity // 2
    route_weight = route_scores / jnp.sum(route_scores, axis=1, keepdims=True)
    flat_ids = expert_ids.reshape(-1)
    onehot = (flat_ids[:, None] == jnp.arange(experts, dtype=jnp.int32)[None, :]).astype(jnp.int32)
    before = jnp.cumsum(onehot, axis=0) - onehot
    rank_in = jnp.sum(before * onehot, axis=1)
    target = 2 * flat_ids + rank_in // half_cap
    position = target * half_cap + rank_in % half_cap
    owners = jnp.arange(rows_dev * top_count, dtype=jnp.int32) // top_count
    outgoing = (
        jnp.zeros((dest_count * half_cap, features), jnp.bfloat16).at[position].set(tokens[owners])
    )
    outgoing = outgoing.reshape(dest_count, half_cap, features)
    arrived = lax.all_to_all(outgoing, ("group", "dev"), split_axis=0, concat_axis=0, tiled=True)
    batch_rows = arrived.reshape(dest_count * half_cap, features)
    partner = partner_2((w_gate[0], w_up[0], w_down[0]), "dev", 0)
    gate_half = jnp.concatenate([w_gate[0], partner[0]], axis=1)
    up_half = jnp.concatenate([w_up[0], partner[1]], axis=1)
    down_half = jnp.concatenate([w_down[0], partner[2]], axis=1)
    full_gate, full_up, full_down = (
        lax.all_gather(gate_half, "pair", axis=1, tiled=True),
        lax.all_gather(up_half, "pair", axis=1, tiled=True),
        lax.all_gather(down_half, "pair", axis=1, tiled=True),
    )
    result = expert_block(batch_rows, full_gate, full_up, full_down)
    answer = result.astype(jnp.bfloat16).reshape(dest_count, half_cap, features)
    returned = lax.all_to_all(answer, ("group", "dev"), split_axis=0, concat_axis=0, tiled=True)
    picked = returned.reshape(dest_count * half_cap, features)[position].astype(jnp.float32)
    weighted = picked * route_weight.reshape(-1)[:, None]
    mixed_out = jnp.sum(weighted.reshape(rows_dev, top_count, features), axis=1)
    return mixed_out.astype(jnp.bfloat16)


def solution(mesh):
    in_specs = (
        P(("parts", "group", "dev", "pair"), None),
        P(("parts", "group", "dev", "pair"), None),
        P(("parts", "group", "dev", "pair"), None),
        P(("group", "dev"), None, "pair"),
        P(("group", "dev"), None, "pair"),
        P(("group", "dev"), None, "pair"),
    )
    out_specs = P(("parts", "group", "dev", "pair"), None)
    few = mesh.shape["group"] == 2 and mesh.shape["pair"] == 2 and 2 <= mesh.shape["dev"] <= 4
    return jax.shard_map(near if few else shards, mesh=mesh, in_specs=in_specs, out_specs=out_specs, check_vma=False)
```

time: 80.4 us -> 69.3 us (0.86)
  local copies, waits for them, and re-layouts: 7.26 us -> 1.67 us
  Pallas kernels: 71.5 us -> 67.4 us
  other arithmetic: 1.36 us -> 0 us
    unnamed x12 -> x1, local copies, waits for them, and re-layouts: 7.26 us -> 1.67 us
    pallas_call x1, Pallas kernels: 71.5 us -> 67.4 us  [near(): pl.pallas_call(functools.partial(fused, n, rows, early, ag_cuts, rs_cuts)...]
    reduce_sum x2 -> x0, other arithmetic: 1.36 us -> none  [the longest x1 0.77 us: near(): route_weight = route_scores / jnp.sum(route_scores, axis=1, keepdims=True)]
where the time goes in v2:
time: 69.3 us; the launch traced here: 69.1 us
  Pallas kernels  67.4 us (97%)
  local copies, waits for them, and re-layouts  1.67 us (2%)
    pallas_call x1, Pallas kernels, near(): pl.pallas_call(functools.partial(fused, n, rows, early, ag_cuts, rs_cuts)...  67.4 us
    unnamed x1, local copies, waits for them, and re-layouts  1.67 us

profile of v2, /device:TPU:0, one launch (start us, length us, event | category | flops | bytes accessed | tf_op | source)
XLA Modules:
  0.0 69.1 jit_solution(10716345988453308419)
XLA Ops:
  0.0 67.4 %shard_map.64 = bf16[64,2048]{1,0:T(8,128)(2,1)} custom-call(bf16[64,2048]{1,0:T(8,128)(2,1)} %tokens.1, s32[2,64]{1,0:T(2,128)} %bitcast.8, f32[2,64]{1,0:T(2,128)} %bitcast.9, bf16[1,192,2048]{2,1,0:T(8,128)(2,1)} %bitcast.5, bf16[1,192,2048]{2,1,0:T(8,128)(2,1)} %bitcast.6, bf16[1,192,2048]{2,1,0:T(8,128)(2,1)} %bitcast.7), custom_call_target="tpu_custom_call" | custom-call | tf_op jit(solution)/shard_map/pallas_call | solution.py:266
  67.4 1.7 %copy.8 = bf16[64,2048]{1,0:T(8,128)(2,1)} copy(bf16[64,2048]{1,0:T(8,128)(2,1)} %shard_map.64) | data formatting | bytes 524288
